TPU v7x, 64 devices: a 2x2x8 block of a 4x4x8 slice. The times are simulated.
64 devices in a mesh: rep: 8 (over x, y, core), dp: 8 (over z).
Axes of the slice: x: 2, y: 2, z: 8, core: 2. Of those that a mesh axis runs over, the one named last changes fastest.
The devices are a block of a 4x4x8 slice.
Arguments:
- a: bfloat16 [64, 4, 4096, 640], P(('rep', 'dp')), parts along dimension 0
- g: bfloat16 [64, 4, 4096, 2432], P(('rep', 'dp')), parts along dimension 0
Outputs:
- output: bfloat16 [32, 640, 2432], P('rep'), parts along dimension 0
There are 8 independent parts. A program takes and returns all parts, laid end to end along the dimension named above; each array names one.
All inputs are finite; a program needn't handle non-finite values.
Results may differ from a plain program's by a relative error of at most 0.012.
Values are sent between devices in bfloat16 or wider.
A program may use at most 768 MiB of HBM per device.

v0:
```python
import jax
import jax.numpy as jnp


def solution(mesh):
    groups = mesh.shape["rep"]

    def step(a, g):
        a, g = (t.reshape(groups, -1, *t.shape[1:]) for t in (a, g))
        sums = jnp.einsum("rsntd,rsntf->rndf", a, g, preferred_element_type=jnp.float32)
        return sums.astype(jnp.bfloat16).reshape(-1, *sums.shape[2:])

    return step
```

profile of v0, /device:TPU:22, one launch (start us, length us, event | category | flops | bytes accessed | tf_op | source)
XLA Modules:
  0.0 554.6 jit_solution(3976160901950240060)
XLA Ops:
  0.0 64.1 %fusion.3 = f32[1,4,640,2432]{3,2,1,0:T(8,128)} fusion(bf16[1,4,4096,2432]{3,2,1,0:T(8,128)(2,1)} %param.1, bf16[1,4,4096,640]{3,2,1,0:T(8,128)(2,1)} %param), kind=kOutput, calls=%fused_computation.4 | convolution fusion | flops 51002736640 | bytes 125566976 | tf_op jit(solution)/rsntd,rsntf->rndf/dot_general | solution.py:10
  64.1 490.5 %all-reduce.2 = bf16[1,4,640,2432]{3,2,1,0:T(8,128)(2,1)} all-reduce(f32[1,4,640,2432]{3,2,1,0:T(8,128)} %fusion.3), channel_id=1, replica_groups=[8,8]<=[64], use_global_device_ids=true, to_apply=%add.clone | all-reduce | flops 6225920 | bytes 37355520 | tf_op jit(solution)/rsntd,rsntf->rndf/dot_general | solution.py:10
where the time goes:
time: 555 us
  blocking collectives  490 us (88%)
  matrix products  64.1 us (12%)
    dot_general x1, blocking collectives, step(): jnp.einsum('rsntd,rsntf->rndf', a, g, preferred_element_type=jnp.float32)  490 us
    dot_general x1, matrix products, step(): jnp.einsum('rsntd,rsntf->rndf', a, g, preferred_element_type=jnp.float32)  64.1 us

commit v1 on v0

v1 whole, which is shorter than its diff:
```python
import functools

import jax
import jax.numpy as jnp
from jax import lax
from jax.experimental import pallas as pl
from jax.experimental.pallas import tpu as pltpu
from jax.sharding import PartitionSpec as P

LANES = 128
WIDE = 2 * LANES
CHUNKS = 4
MESH = pl.DeviceIdType.MESH


def kernel(n, a_ref, g_ref, out_ref, land, a_t, g_buf, part, moving, whole,
           a_sem, g_sem, send_sem, recv_sem, out_sem):
    matrices, tokens, d_model = a_ref.shape
    blocks = g_ref.shape[2] // LANES
    pairs = matrices * blocks // 2
    stages = pairs // 2
    rows = d_model // n
    hold = part.shape[0]
    step_rows = tokens // CHUNKS
    last = 2 * n - 2
    me = lax.axis_index("dp")
    beside = (lax.rem(me + 1, n), lax.rem(me + n - 1, n))

    def owner(d, away):
        sign = 1 - 2 * d
        return lax.rem(me - sign * away + 2 * n, n)

    def at(c):
        return pl.ds(pl.multiple_of(c * rows, rows), rows)

    def a_copy(k):
        slot = lax.rem(k, CHUNKS)
        return pltpu.make_async_copy(
            a_ref.at[k // CHUNKS, pl.ds(pl.multiple_of(slot * step_rows, step_rows), step_rows)],
            land.at[slot], a_sem.at[slot])

    def place(b):
        return b // blocks, pl.multiple_of(lax.rem(b, blocks) * LANES, LANES)

    def crosses(p):
        return lax.rem(2 * p, blocks) == blocks - 1

    def g_copy(p, slot):
        m, col = place(2 * p)
        return pltpu.make_async_copy(
            g_ref.at[m, :, pl.ds(col, WIDE)], g_buf.at[slot], g_sem.at[slot])

    def g_start(p):
        slot = lax.rem(p, 3)

        @pl.when(jnp.logical_not(crosses(p)))
        def _():
            g_copy(p, slot).start()

        @pl.when(crosses(p))
        def _():
            for i in range(2):
                m, col = place(2 * p + i)
                pltpu.make_async_copy(
                    g_ref.at[m, :, pl.ds(col, LANES)],
                    g_buf.at[slot, :, pl.ds(i * LANES, LANES)], g_sem.at[slot]).start()

    def turn(k):
        a_copy(k).wait()
        slot = lax.rem(k, CHUNKS)
        half = step_rows // 2
        for i in range(2):
            a_t[lax.rem(k // CHUNKS, 2), :,
                pl.ds(pl.multiple_of(slot * step_rows + i * half, half), half)] = (
                    land[slot, pl.ds(i * half, half)].T)

        @pl.when(k + CHUNKS < matrices * CHUNKS)
        def _():
            a_copy(k + CHUNKS).start()

    def compute(q, d):
        p = 2 * q + d
        slot = lax.rem(p, 3)
        keep = lax.rem(q, hold)
        pltpu.make_async_copy(
            g_ref.at[0, :, pl.ds(0, WIDE)], g_buf.at[slot], g_sem.at[slot]).wait()

        @pl.when(p + 2 < pairs)
        def _():
            g_start(p + 2)

        first = lax.rem(2 * p // blocks, 2)

        @pl.when(jnp.logical_not(crosses(p)))
        def _():
            part[keep, d] = jnp.dot(
                a_t[first], g_buf[slot], preferred_element_type=jnp.float32)

        @pl.when(crosses(p))
        def _():
            for i in range(2):
                side = pl.ds(i * LANES, LANES)
                part[keep, d, :, side] = jnp.dot(
                    a_t[lax.rem(first + i, 2)], g_buf[slot, :, side],
                    preferred_element_type=jnp.float32)

    def message(q, d, t, source, target, to):
        return pltpu.make_async_remote_copy(
            src_ref=source, dst_ref=target,
            send_sem=send_sem.at[d, q, lax.rem(t, 2)],
            recv_sem=recv_sem.at[d, q, t],
            device_id={"dp": to}, device_id_type=MESH)

    def any_message(q, d, t):
        ref = moving.at[d, q, 0]
        return message(q, d, t, ref, ref, beside[0])

    def begin(q, d):
        c = owner(d, 1)
        to = lax.rem(me + 1 - 2 * d + n, n)
        moving[d, q, 0] = part[lax.rem(q, hold), d, at(c)].astype(jnp.bfloat16)
        message(q, d, 0, moving.at[d, q, 0], moving.at[d, q, 1], to).start()

    def reduce_step(q, t):
        for d in range(2):
            any_message(q, d, t - 1).wait_recv()
            c = owner(d, 1 + t)
            so_far = moving[d, q, t].astype(jnp.float32)
            moving[d, q, t] = (so_far + part[lax.rem(q, hold), d, at(c)]).astype(jnp.bfloat16)

            @pl.when(t >= 2)
            def _():
                any_message(q, d, t).wait_send()

            message(q, d, t, moving.at[d, q, t], moving.at[d, q, t + 1], beside[d]).start()

    def finish_step(q):
        t = n - 1
        for d in range(2):
            any_message(q, d, t - 1).wait_recv()
            so_far = moving[d, q, t].astype(jnp.float32)
            mine = whole.at[2 * q + d, at(me)]
            mine[...] = (so_far + part[lax.rem(q, hold), d, at(me)]).astype(jnp.bfloat16)
            any_message(q, d, t).wait_send()
            message(q, d, t, mine, mine, beside[d]).start()

    def gather_step(q, t):
        for d in range(2):
            any_message(q, d, t - 1).wait_recv()
            block = whole.at[2 * q + d, at(owner(d, t - n + 1))]
            any_message(q, d, t).wait_send()
            message(q, d, t, block, block, beside[d]).start()

    def out_copy(p, i, width):
        m, col = place(2 * p + i)
        return pltpu.make_async_copy(
            whole.at[p, :, pl.ds(i * LANES, width)],
            out_ref.at[m, :, pl.ds(col, width)], out_sem.at[p])

    def close(q):
        for d in range(2):
            p = 2 * q + d
            any_message(q, d, last - 1).wait_recv()
            any_message(q, d, 0).wait_send()
            any_message(q, d, 1).wait_send()

            @pl.when(jnp.logical_not(crosses(p)))
            def _():
                out_copy(p, 0, WIDE).start()

            @pl.when(crosses(p))
            def _():
                for i in range(2):
                    out_copy(p, i, LANES).start()

    for k in range(CHUNKS):
        a_copy(k).start()
    for p in range(2):
        g_start(p)
    barrier = pltpu.get_barrier_semaphore()
    for to in beside:
        pl.semaphore_signal(barrier, inc=1, device_id={"dp": to}, device_id_type=MESH)
    pl.semaphore_wait(barrier, 2)

    def first_chunks(k, _):
        turn(k)
        return 0

    lax.fori_loop(0, CHUNKS, first_chunks, 0)

    def tick(r, _):
        @pl.when(jnp.logical_and(lax.rem(r, 5) != 0, r < 15))
        def _():
            turn(r + 3 - r // 5)

        @pl.when(r < stages)
        def _():
            def one(d, _):
                compute(r, d)
                begin(r, d)
                return 0

            lax.fori_loop(0, 2, one, 0)

        def bounds(lo, hi):
            return jnp.maximum(lo, r - stages + 1), jnp.minimum(hi, r) + 1

        def red(t, _):
            reduce_step(r - t, t)
            return 0

        lax.fori_loop(*bounds(1, n - 2), red, 0)

        @pl.when(jnp.logical_and(r >= n - 1, r - (n - 1) < stages))
        def _():
            finish_step(r - (n - 1))

        def gat(t, _):
            gather_step(r - t, t)
            return 0

        lax.fori_loop(*bounds(n, last - 1), gat, 0)

        @pl.when(jnp.logical_and(r >= last, r - last < stages))
        def _():
            close(r - last)

        return 0

    lax.fori_loop(0, stages + last, tick, 0)

    def drain(p, _):
        pltpu.make_async_copy(
            whole.at[0], out_ref.at[0, :, pl.ds(0, WIDE)], out_sem.at[p]).wait()
        return 0

    lax.fori_loop(0, pairs, drain, 0)


def solution(mesh):
    n = mesh.shape["dp"]

    def local(a, g):
        a, g = a[0], g[0]
        matrices, tokens, d_model = a.shape
        ff = g.shape[2]
        pairs = matrices * ff // WIDE
        stages = pairs // 2
        rows = d_model // n
        steps = 2 * n - 2
        call = pl.pallas_call(
            functools.partial(kernel, n),
            out_shape=jax.ShapeDtypeStruct((matrices, d_model, ff), jnp.bfloat16),
            in_specs=[pl.BlockSpec(memory_space=pl.ANY)] * 2,
            out_specs=pl.BlockSpec(memory_space=pl.ANY),
            scratch_shapes=[
                pltpu.VMEM((CHUNKS, tokens // CHUNKS, d_model), jnp.bfloat16),
                pltpu.VMEM((2, d_model, tokens), jnp.bfloat16),
                pltpu.VMEM((3, tokens, WIDE), jnp.bfloat16),
                pltpu.VMEM((n, 2, d_model, WIDE), jnp.float32),
                pltpu.VMEM((2, stages, n, rows, WIDE), jnp.bfloat16),
                pltpu.VMEM((pairs, d_model, WIDE), jnp.bfloat16),
                pltpu.SemaphoreType.DMA((CHUNKS,)),
                pltpu.SemaphoreType.DMA((3,)),
                pltpu.SemaphoreType.DMA((2, stages, 2)),
                pltpu.SemaphoreType.DMA((2, stages, steps)),
                pltpu.SemaphoreType.DMA((pairs,)),
            ],
            compiler_params=pltpu.CompilerParams(
                collective_id=0, has_side_effects=True, vmem_limit_bytes=67043328),
            cost_estimate=pl.CostEstimate(
                flops=2 * matrices * tokens * d_model * ff,
                bytes_accessed=2 * matrices * (tokens * (d_model + ff) + d_model * ff),
                transcendentals=0),
        )
        return call(a, g)

    return jax.shard_map(
        local, mesh=mesh, in_specs=(P(("rep", "dp")), P(("rep", "dp"))),
        out_specs=P("rep"), check_vma=False)
```

time: 555 us -> 275 us (0.50)
  blocking collectives: 490 us -> 0 us
  Pallas kernels: 0 us -> 265 us
  matrix products: 64.1 us -> 0 us
  local copies, waits for them, and re-layouts: 0 us -> 10.4 us
    dot_general x1 -> x0, blocking collectives: 490 us -> none  [step(): jnp.einsum('rsntd,rsntf->rndf', a, g, preferred_element_type=jnp.float32)]
    pallas_call x0 -> x1, Pallas kernels: none -> 265 us  [local(): return call(a, g)]
    dot_general x1 -> x0, matrix products: 64.1 us -> none  [step(): jnp.einsum('rsntd,rsntf->rndf', a, g, preferred_element_type=jnp.float32)]
    unnamed x0 -> x1, local copies, waits for them, and re-layouts: none -> 10.4 us
where the time goes in v1:
time: 275 us
  Pallas kernels  265 us (96%)
  local copies, waits for them, and re-layouts  10.4 us (4%)
    pallas_call x1, Pallas kernels, local(): return call(a, g)  265 us
    unnamed x1, local copies, waits for them, and re-layouts  10.4 us

profile of v1, /device:TPU:22, one launch (start us, length us, event | category | flops | bytes accessed | tf_op | source)
XLA Modules:
  0.0 275.2 jit_solution(13879914379674682965)
XLA Ops:
  0.0 264.7 %shard_map.28 = bf16[4,640,2432]{2,1,0:T(8,128)(2,1)} custom-call(bf16[4,4096,640]{2,1,0:T(8,128)(2,1)} %bitcast.2, bf16[4,4096,2432]{2,1,0:T(8,128)(2,1)} %bitcast.1.g_ref), custom_call_target="tpu_custom_call" | custom-call | flops 51002736640 | bytes 113115136 | tf_op jit(solution)/shard_map/pallas_call | solution.py:276
  264.7 10.4 %copy.4 = bf16[4,640,2432]{2,1,0:T(8,128)(2,1)} copy(bf16[4,640,2432]{2,1,0:T(8,128)(2,1)} %shard_map.28) | data formatting | bytes 24903680

commit v2 on v0

v2 whole, which is shorter than its diff:
```python
import functools

import jax
import jax.numpy as jnp
from jax import lax
from jax.experimental import pallas as pl
from jax.experimental.pallas import tpu as pltpu
from jax.sharding import PartitionSpec as P

LANES = 128
WIDE = 2 * LANES
CHUNKS = 4
TURNS = (6, 7, 8, 9, 12, 14, 16, 18, 21, 23, 25, 27)
GROUPS = (1, 1, 1, 1, 1, 1, 2, 2, 4, 8, 8, 8)
MESH = pl.DeviceIdType.MESH


def plan(groups, steps, tile=1.8, turn=0.4, lag=1.8, wire=0.44, gap=0.036, depth=4.0):
    now, link, after, order = 0.0, 0.0, [], [[]]
    ends = [sum(groups[:i + 1]) for i in range(len(groups))]
    p, tiles = 0, sum(groups)
    while p < tiles or after:
        ready = [x for x in after if x[0] <= now and (link - now < depth or x[1] == steps)]
        if ready:
            x = min(ready, key=lambda x: (x[1], x[0], x[2]))
            after.remove(x)
            _, t, i = x
            order[-1].append((i, t))
            now += 0.06 + 0.12 * groups[i] * (t <= steps // 2)
            if t < steps:
                link = max(link, now) + groups[i] * wire + gap
                after.append((link + lag, t + 1, i))
        elif p < tiles:
            now += tile + turn * (p in TURNS)
            p += 1
            order.append([])
            if p in ends:
                after.append((now, 0, ends.index(p)))
        else:
            now = min(max(t, link - depth + 1e-6) if s < steps else t for t, s, _ in after)
    return order[1:]


def kernel(n, groups, a_ref, g_ref, whole, land, a_t, g_buf, part,
           a_sem, g_sem, first_sem, send_sem, recv_sem):
    matrices, tokens, d_model = a_ref.shape
    blocks = g_ref.shape[2] // LANES
    pairs = matrices * blocks // 2
    rows = d_model // n
    step_rows = tokens // CHUNKS
    last = 2 * n - 2
    begins = [sum(groups[:i]) for i in range(len(groups))]
    me = lax.axis_index("dp")

    def owner(d, away):
        return lax.rem(me - (1 - 2 * d) * away + 2 * n, n)

    def k_rows(k):
        return pl.ds(pl.multiple_of(lax.rem(k, CHUNKS) * step_rows, step_rows), step_rows)

    def a_copy(k):
        slot = lax.rem(k, CHUNKS)
        return pltpu.make_async_copy(
            a_ref.at[k // CHUNKS, k_rows(k)], land.at[slot], a_sem.at[slot])

    def first_g(k):
        return pltpu.make_async_copy(
            g_ref.at[0, k_rows(k), pl.ds(0, WIDE)], g_buf.at[0, k_rows(k)], first_sem.at[k])

    def place(b):
        return b // blocks, pl.multiple_of(lax.rem(b, blocks) * LANES, LANES)

    def crosses(p):
        return lax.rem(2 * p, blocks) == blocks - 1

    def g_start(p):
        slot = lax.rem(p, 3)

        @pl.when(jnp.logical_not(crosses(p)))
        def _():
            m, col = place(2 * p)
            pltpu.make_async_copy(
                g_ref.at[m, :, pl.ds(col, WIDE)], g_buf.at[slot], g_sem.at[slot]).start()

        @pl.when(crosses(p))
        def _():
            for i in range(2):
                m, col = place(2 * p + i)
                pltpu.make_async_copy(
                    g_ref.at[m, :, pl.ds(col, LANES)],
                    g_buf.at[slot, :, pl.ds(i * LANES, LANES)], g_sem.at[slot]).start()

    def turn(k):
        a_copy(k).wait()
        slot = lax.rem(k, CHUNKS)
        half = step_rows // 2
        for i in range(2):
            a_t[lax.rem(k // CHUNKS, 2), :,
                pl.ds(pl.multiple_of(slot * step_rows + i * half, half), half)] = (
                    land[slot, pl.ds(i * half, half)].T)

    def compute(p):
        slot = lax.rem(p, 3)
        pltpu.make_async_copy(
            g_ref.at[0, :, pl.ds(0, WIDE)], g_buf.at[slot], g_sem.at[slot]).wait()

        @pl.when(p + 2 < pairs)
        def _():
            g_start(p + 2)

        first = lax.rem(2 * p // blocks, 2)

        @pl.when(jnp.logical_not(crosses(p)))
        def _():
            both = jnp.dot(a_t[first], g_buf[slot], preferred_element_type=jnp.float32)
            part[p, 0] = both[:, :LANES]
            part[p, 1] = both[:, LANES:]

        @pl.when(crosses(p))
        def _():
            for i in range(2):
                part[p, i] = jnp.dot(
                    a_t[lax.rem(first + i, 2)], g_buf[slot, :, pl.ds(i * LANES, LANES)],
                    preferred_element_type=jnp.float32)

    def message(i, d, t, block, to):
        return pltpu.make_async_remote_copy(
            src_ref=block, dst_ref=block,
            send_sem=send_sem.at[d, i, t % 2], recv_sem=recv_sem.at[d, i, t],
            device_id={"dp": to}, device_id_type=MESH)

    def carry(i, t):
        q, size = begins[i], groups[i]

        def one(d, _):
            def message_of(s):
                return message(i, d, s, whole.at[d, 0, pl.ds(q, size)], me)

            if t > 0:
                message_of(t - 1).wait_recv()
            c = owner(d, 1 + t if t < n else t - n + 1)
            if t < n:
                mine = pl.ds(pl.multiple_of(c * rows, rows), rows)

                def add(j, _):
                    term = part[q + j, d, mine]
                    if t > 0:
                        term = whole[d, c, q + j].astype(jnp.float32) + term
                    whole[d, c, q + j] = term.astype(jnp.bfloat16)
                    return 0

                lax.fori_loop(0, size, add, 0)
            if t >= 2:
                message_of(t - 2).wait_send()
            if t < last:
                to = lax.rem(me + 1 - 2 * d + n, n)
                message(i, d, t, whole.at[d, c, pl.ds(q, size)], to).start()
            else:
                message_of(t - 1).wait_send()
            return 0

        lax.fori_loop(0, 2, one, 0)

    for k in range(CHUNKS):
        a_copy(k).start()
        first_g(k).start()
    barrier = pltpu.get_barrier_semaphore()
    beside = (lax.rem(me + 1, n), lax.rem(me + n - 1, n))
    for to in beside:
        pl.semaphore_signal(barrier, inc=1, device_id={"dp": to}, device_id_type=MESH)
    part[0] = jnp.zeros(part.shape[1:], jnp.float32)

    def first_tile(k, _):
        turn(k)
        first_g(k).wait()

        @pl.when(lax.rem(k, 2) == 1)
        def _():
            g_start(1 + k // 2)

        both = jnp.dot(a_t[0, :, k_rows(k)], g_buf[0, k_rows(k)],
                       preferred_element_type=jnp.float32)
        part[0, 0] += both[:, :LANES]
        part[0, 1] += both[:, LANES:]
        return 0

    lax.fori_loop(0, CHUNKS, first_tile, 0)
    pl.semaphore_wait(barrier, 2)
    order = plan(groups, last)
    for i, t in order[0]:
        carry(i, t)

    def tile(p, _):
        @pl.when(p <= CHUNKS)
        def _():
            a_copy(CHUNKS + p - 1).start()

        k = CHUNKS + sum((p > x).astype(jnp.int32) for x in TURNS)
        due = functools.reduce(jnp.logical_or, [p == x for x in TURNS])

        @pl.when(due)
        def _():
            turn(k)

            @pl.when(k + CHUNKS < matrices * CHUNKS)
            def _():
                a_copy(k + CHUNKS).start()

        compute(p)
        for x in range(1, pairs - 1):
            if order[x]:
                @pl.when(p == x)
                def _():
                    for i, t in order[x]:
                        carry(i, t)

        return 0

    lax.fori_loop(1, pairs, tile, 0)
    for i, t in order[-1]:
        carry(i, t)


def put(n, whole, out_ref, sem):
    blocks = out_ref.shape[3] // LANES

    def one(p, wait):
        for d in range(2):
            b = 2 * p + d
            col = pl.multiple_of(lax.rem(b, blocks) * LANES, LANES)
            copy = pltpu.make_async_copy(
                whole.at[d, :, p], out_ref.at[b // blocks, :, :, pl.ds(col, LANES)],
                sem.at[d, p])
            copy.wait() if wait else copy.start()
        return 0

    lax.fori_loop(0, whole.shape[2], lambda p, _: one(p, False), 0)
    lax.fori_loop(0, whole.shape[2], lambda p, _: one(p, True), 0)


def solution(mesh):
    n = mesh.shape["dp"]

    def local(a, g):
        a, g = a[0], g[0]
        matrices, tokens, d_model = a.shape
        ff = g.shape[2]
        pairs = matrices * ff // WIDE
        rows = d_model // n
        whole = pl.pallas_call(
            functools.partial(kernel, n, GROUPS),
            out_shape=pltpu.VMEM((2, n, pairs, rows, LANES), jnp.bfloat16),
            in_specs=[pl.BlockSpec(memory_space=pl.ANY)] * 2,
            out_specs=pl.BlockSpec(memory_space=pltpu.VMEM),
            scratch_shapes=[
                pltpu.VMEM((CHUNKS, tokens // CHUNKS, d_model), jnp.bfloat16),
                pltpu.VMEM((2, d_model, tokens), jnp.bfloat16),
                pltpu.VMEM((3, tokens, WIDE), jnp.bfloat16),
                pltpu.VMEM((pairs, 2, d_model, LANES), jnp.float32),
                pltpu.SemaphoreType.DMA((CHUNKS,)),
                pltpu.SemaphoreType.DMA((3,)),
                pltpu.SemaphoreType.DMA((CHUNKS,)),
                pltpu.SemaphoreType.DMA((2, len(GROUPS), 2)),
                pltpu.SemaphoreType.DMA((2, len(GROUPS), 2 * n - 2)),
            ],
            compiler_params=pltpu.CompilerParams(
                collective_id=0, has_side_effects=True, vmem_limit_bytes=50 << 20),
            cost_estimate=pl.CostEstimate(
                flops=2 * matrices * tokens * d_model * ff,
                bytes_accessed=2 * matrices * tokens * (d_model + ff),
                transcendentals=0),
        )(a, g)
        out = pl.pallas_call(
            functools.partial(put, n),
            out_shape=jax.ShapeDtypeStruct((matrices, n, rows, ff), jnp.bfloat16),
            in_specs=[pl.BlockSpec(memory_space=pltpu.VMEM)],
            out_specs=pl.BlockSpec(memory_space=pl.ANY),
            scratch_shapes=[pltpu.SemaphoreType.DMA((2, pairs))],
            compiler_params=pltpu.CompilerParams(vmem_limit_bytes=16 << 20),
        )(whole)
        return out.reshape(matrices, d_model, ff)

    return jax.shard_map(
        local, mesh=mesh, in_specs=(P(("rep", "dp")), P(("rep", "dp"))),
        out_specs=P("rep"), check_vma=False)
```

time: 555 us -> 266 us (0.48)
  blocking collectives: 490 us -> 0 us
  Pallas kernels: 0 us -> 266 us
  matrix products: 64.1 us -> 0 us
    dot_general x1 -> x0, blocking collectives: 490 us -> none  [step(): jnp.einsum('rsntd,rsntf->rndf', a, g, preferred_element_type=jnp.float32)]
    pallas_call x0 -> x2, Pallas kernels: none -> 266 us  [the longest x1 260 us: local(): pl.pallas_call(functools.partial(kernel, n, GROUPS), out_shape=pltpu.VMEM...]
    dot_general x1 -> x0, matrix products: 64.1 us -> none  [step(): jnp.einsum('rsntd,rsntf->rndf', a, g, preferred_element_type=jnp.float32)]
where the time goes in v2:
time: 266 us
  Pallas kernels  266 us (100%)
    pallas_call x1, Pallas kernels, local(): pl.pallas_call(functools.partial(kernel, n, GROUPS), out_shape=pltpu.VMEM...  260 us

profile of v2, /device:TPU:22, one launch (start us, length us, event | category | flops | bytes accessed | tf_op | source)
XLA Modules:
  0.0 265.6 jit_solution(8255666512609674257)
XLA Ops:
  0.0 260.5 %shard_map.28.whole = bf16[2,8,38,80,128]{4,3,2,1,0:T(8,128)(2,1)S(1)} custom-call(bf16[4,4096,640]{2,1,0:T(8,128)(2,1)} %bitcast.3, bf16[4,4096,2432]{2,1,0:T(8,128)(2,1)} %bitcast.1.g_ref), custom_call_target="tpu_custom_call" | custom-call | flops 51002736640 | bytes 100663296 | tf_op jit(solution)/shard_map/pallas_call | solution.py:250
  260.5 5.2 %shard_map.29 = bf16[4,8,80,2432]{3,2,1,0:T(8,128)(2,1)} custom-call(bf16[2,8,38,80,128]{4,3,2,1,0:T(8,128)(2,1)S(1)} %shard_map.28.whole), custom_call_target="tpu_custom_call" | custom-call | tf_op jit(solution)/shard_map/pallas_call | solution.py:273

commit v3 on v2

--- a/solution.py
+++ b/solution.py
@@ -12,37 +12,57 @@
 CHUNKS = 4
 TURNS = (6, 7, 8, 9, 12, 14, 16, 18, 21, 23, 25, 27)
 GROUPS = (1, 1, 1, 1, 1, 1, 2, 2, 4, 8, 8, 8)
+FRONT = 6
 MESH = pl.DeviceIdType.MESH
 
 
-def plan(groups, steps, tile=1.8, turn=0.4, lag=1.8, wire=0.44, gap=0.036, depth=4.0):
-    now, link, after, order = 0.0, 0.0, [], [[]]
+def plan(groups, n, work=0.6, half=1.0, turn=0.36, load=0.66, lag=1.5, wire=0.44, gap=0.03,
+         depth=4.0):
+    steps = 2 * n - 2
     ends = [sum(groups[:i + 1]) for i in range(len(groups))]
-    p, tiles = 0, sum(groups)
-    while p < tiles or after:
-        ready = [x for x in after if x[0] <= now and (link - now < depth or x[1] == steps)]
+    rounds = n // 2
+    pieces = [(r, p) for r in range(rounds) for p in range(FRONT)]
+    pieces += [(h, p) for p in range(FRONT, ends[-1]) for h in range(2)]
+    now, link, after, order, done = 0.0, 0.0, [], [], [0] * FRONT
+    held = {}
+    x = 0
+    while x < len(pieces) or after:
+        ready = [e for e in after if e[0] <= now and (link - now < depth or e[1] == steps)
+                 and not (e[2] < FRONT and e[1] < n and need(e[1], n) >= done[e[2]])]
         if ready:
-            x = min(ready, key=lambda x: (x[1], x[0], x[2]))
-            after.remove(x)
-            _, t, i = x
+            e = min(ready, key=lambda e: (e[1], e[0], e[2]))
+            after.remove(e)
+            _, t, i = e
             order[-1].append((i, t))
-            now += 0.06 + 0.12 * groups[i] * (t <= steps // 2)
+            now += 0.06 + 0.08 * groups[i] * (t < n)
             if t < steps:
                 link = max(link, now) + groups[i] * wire + gap
                 after.append((link + lag, t + 1, i))
-        elif p < tiles:
-            now += tile + turn * (p in TURNS)
-            p += 1
+        elif x < len(pieces):
+            r, p = pieces[x]
+            if p < FRONT:
+                now = max(now, load * p) + work
+                done[p] = r + 1
+                if r == 0:
+                    after.append((now, 0, p))
+            else:
+                now += half + turn * (p in TURNS and r == 0)
+                if r == 1 and p + 1 in ends:
+                    after.append((now, 0, ends.index(p + 1)))
+            x += 1
             order.append([])
-            if p in ends:
-                after.append((now, 0, ends.index(p)))
         else:
             now = min(max(t, link - depth + 1e-6) if s < steps else t for t, s, _ in after)
-    return order[1:]
+    return order
+
+
+def need(t, n):
+    away = min(1 + t, n - 1 - t)
+    return away - 1 if 0 < away < n // 2 else n // 2 - 1
 
 
 def kernel(n, groups, a_ref, g_ref, whole, land, a_t, g_buf, part,
-           a_sem, g_sem, first_sem, send_sem, recv_sem):
+           a_sem, g_sem, send_sem, recv_sem):
     matrices, tokens, d_model = a_ref.shape
     blocks = g_ref.shape[2] // LANES
     pairs = matrices * blocks // 2
@@ -63,10 +83,6 @@
         return pltpu.make_async_copy(
             a_ref.at[k // CHUNKS, k_rows(k)], land.at[slot], a_sem.at[slot])
 
-    def first_g(k):
-        return pltpu.make_async_copy(
-            g_ref.at[0, k_rows(k), pl.ds(0, WIDE)], g_buf.at[0, k_rows(k)], first_sem.at[k])
-
     def place(b):
         return b // blocks, pl.multiple_of(lax.rem(b, blocks) * LANES, LANES)
 
@@ -74,7 +90,7 @@
         return lax.rem(2 * p, blocks) == blocks - 1
 
     def g_start(p):
-        slot = lax.rem(p, 3)
+        slot = lax.rem(p, FRONT)
 
         @pl.when(jnp.logical_not(crosses(p)))
         def _():
@@ -99,28 +115,39 @@
                 pl.ds(pl.multiple_of(slot * step_rows + i * half, half), half)] = (
                     land[slot, pl.ds(i * half, half)].T)
 
-    def compute(p):
-        slot = lax.rem(p, 3)
+    def g_wait(p):
+        slot = lax.rem(p, FRONT)
         pltpu.make_async_copy(
             g_ref.at[0, :, pl.ds(0, WIDE)], g_buf.at[slot], g_sem.at[slot]).wait()
 
-        @pl.when(p + 2 < pairs)
-        def _():
-            g_start(p + 2)
-
+    def at(c):
+        return pl.ds(pl.multiple_of(c * rows, rows), rows)
+
+    def front(r, p):
+        end = r == n // 2 - 1
+        ones = (owner(0, 1 + r), jnp.where(end, me, owner(1, 1 + r)))
+        left = jnp.concatenate([a_t[0, at(c)] for c in ones], axis=0)
+        both = jnp.dot(left, g_buf[p], preferred_element_type=jnp.float32)
+        for i, c in enumerate(ones):
+            for d in range(2):
+                part[p, d, at(c)] = both[i * rows:(i + 1) * rows, d * LANES:(d + 1) * LANES]
+
+    def compute(p, h):
+        slot = lax.rem(p, FRONT)
         first = lax.rem(2 * p // blocks, 2)
+        some = pl.ds(pl.multiple_of(h * (d_model // 2), d_model // 2), d_model // 2)
 
         @pl.when(jnp.logical_not(crosses(p)))
         def _():
-            both = jnp.dot(a_t[first], g_buf[slot], preferred_element_type=jnp.float32)
-            part[p, 0] = both[:, :LANES]
-            part[p, 1] = both[:, LANES:]
+            both = jnp.dot(a_t[first, some], g_buf[slot], preferred_element_type=jnp.float32)
+            part[p, 0, some] = both[:, :LANES]
+            part[p, 1, some] = both[:, LANES:]
 
         @pl.when(crosses(p))
         def _():
             for i in range(2):
-                part[p, i] = jnp.dot(
-                    a_t[lax.rem(first + i, 2)], g_buf[slot, :, pl.ds(i * LANES, LANES)],
+                part[p, i, some] = jnp.dot(
+                    a_t[lax.rem(first + i, 2), some], g_buf[slot, :, pl.ds(i * LANES, LANES)],
                     preferred_element_type=jnp.float32)
 
     def message(i, d, t, block, to):
@@ -140,10 +167,8 @@
                 message_of(t - 1).wait_recv()
             c = owner(d, 1 + t if t < n else t - n + 1)
             if t < n:
-                mine = pl.ds(pl.multiple_of(c * rows, rows), rows)
-
                 def add(j, _):
-                    term = part[q + j, d, mine]
+                    term = part[q + j, d, at(c)]
                     if t > 0:
                         term = whole[d, c, q + j].astype(jnp.float32) + term
                     whole[d, c, q + j] = term.astype(jnp.bfloat16)
@@ -163,61 +188,97 @@
 
     for k in range(CHUNKS):
         a_copy(k).start()
-        first_g(k).start()
+    g_start(0)
     barrier = pltpu.get_barrier_semaphore()
     beside = (lax.rem(me + 1, n), lax.rem(me + n - 1, n))
     for to in beside:
         pl.semaphore_signal(barrier, inc=1, device_id={"dp": to}, device_id_type=MESH)
-    part[0] = jnp.zeros(part.shape[1:], jnp.float32)
-
-    def first_tile(k, _):
+
+    def first_matrix(k, _):
         turn(k)
-        first_g(k).wait()
-
-        @pl.when(lax.rem(k, 2) == 1)
-        def _():
-            g_start(1 + k // 2)
-
-        both = jnp.dot(a_t[0, :, k_rows(k)], g_buf[0, k_rows(k)],
-                       preferred_element_type=jnp.float32)
-        part[0, 0] += both[:, :LANES]
-        part[0, 1] += both[:, LANES:]
+
+        @pl.when(k >= CHUNKS - 2)
+        def _():
+            g_start(1 + k - (CHUNKS - 2))
+
         return 0
 
-    lax.fori_loop(0, CHUNKS, first_tile, 0)
+    lax.fori_loop(0, CHUNKS, first_matrix, 0)
     pl.semaphore_wait(barrier, 2)
-    order = plan(groups, last)
-    for i, t in order[0]:
-        carry(i, t)
-
-    def tile(p, _):
-        @pl.when(p <= CHUNKS)
-        def _():
-            a_copy(CHUNKS + p - 1).start()
-
-        k = CHUNKS + sum((p > x).astype(jnp.int32) for x in TURNS)
-        due = functools.reduce(jnp.logical_or, [p == x for x in TURNS])
-
-        @pl.when(due)
-        def _():
-            turn(k)
-
-            @pl.when(k + CHUNKS < matrices * CHUNKS)
-            def _():
-                a_copy(k + CHUNKS).start()
-
-        compute(p)
-        for x in range(1, pairs - 1):
-            if order[x]:
-                @pl.when(p == x)
+    order = plan(groups, n)
+    early = n // 2 * FRONT
+
+    def follow(x, lo, hi):
+        if hi - lo == 1:
+            for i, t in order[lo]:
+                carry(i, t)
+        elif any(order[lo:hi]):
+            mid = (lo + hi) // 2
+
+            @pl.when(x < mid)
+            def _():
+                follow(x, lo, mid)
+
+            @pl.when(x >= mid)
+            def _():
+                follow(x, mid, hi)
+
+    def front_piece(x, _):
+        r, p = x // FRONT, lax.rem(x, FRONT)
+
+        @pl.when(r == 0)
+        def _():
+            g_wait(p)
+
+            @pl.when(p + 3 < FRONT)
+            def _():
+                g_start(p + 3)
+
+        @pl.when(jnp.logical_and(r == 1, p < CHUNKS))
+        def _():
+            a_copy(CHUNKS + p).start()
+
+        front(r, p)
+
+        @pl.when(jnp.logical_and(r == n // 2 - 1, p < FRONT - 1))
+        def _():
+            g_start(FRONT + p)
+
+        follow(x, 0, early)
+        return 0
+
+    lax.fori_loop(0, early, front_piece, 0)
+
+    def piece(x, _):
+        p, h = FRONT + x // 2, lax.rem(x, 2)
+
+        @pl.when(h == 0)
+        def _():
+            k = CHUNKS + sum((p > y).astype(jnp.int32) for y in TURNS)
+            due = functools.reduce(jnp.logical_or, [p == y for y in TURNS])
+
+            @pl.when(due)
+            def _():
+                turn(k)
+
+                @pl.when(k + CHUNKS < matrices * CHUNKS)
                 def _():
-                    for i, t in order[x]:
-                        carry(i, t)
-
+                    a_copy(k + CHUNKS).start()
+
+            @pl.when(p + FRONT - 1 < pairs)
+            def _():
+                g_start(p + FRONT - 1)
+
+            g_wait(p)
+
+        compute(p, h)
+        follow(early + x, early, len(order))
         return 0
 
-    lax.fori_loop(1, pairs, tile, 0)
-    for i, t in order[-1]:
+    late = order[-1]
+    order[-1] = []
+    lax.fori_loop(0, 2 * (pairs - FRONT), piece, 0)
+    for i, t in late:
         carry(i, t)
 
 
@@ -255,16 +316,15 @@
             scratch_shapes=[
                 pltpu.VMEM((CHUNKS, tokens // CHUNKS, d_model), jnp.bfloat16),
                 pltpu.VMEM((2, d_model, tokens), jnp.bfloat16),
-                pltpu.VMEM((3, tokens, WIDE), jnp.bfloat16),
+                pltpu.VMEM((FRONT, tokens, WIDE), jnp.bfloat16),
                 pltpu.VMEM((pairs, 2, d_model, LANES), jnp.float32),
                 pltpu.SemaphoreType.DMA((CHUNKS,)),
-                pltpu.SemaphoreType.DMA((3,)),
-                pltpu.SemaphoreType.DMA((CHUNKS,)),
+                pltpu.SemaphoreType.DMA((FRONT,)),
                 pltpu.SemaphoreType.DMA((2, len(GROUPS), 2)),
                 pltpu.SemaphoreType.DMA((2, len(GROUPS), 2 * n - 2)),
             ],
             compiler_params=pltpu.CompilerParams(
-                collective_id=0, has_side_effects=True, vmem_limit_bytes=50 << 20),
+                collective_id=0, has_side_effects=True, vmem_limit_bytes=52 << 20),
             cost_estimate=pl.CostEstimate(
                 flops=2 * matrices * tokens * d_model * ff,
                 bytes_accessed=2 * matrices * tokens * (d_model + ff),

time: 266 us -> 264 us (level)
  no operation moved by 1% of the time
where the time goes in v3:
time: 264 us
  Pallas kernels  264 us (100%)
    pallas_call x1, Pallas kernels, local(): pl.pallas_call(functools.partial(kernel, n, GROUPS), out_shape=pltpu.VMEM...  258 us

profile of v3, /device:TPU:22, one launch (start us, length us, event | category | flops | bytes accessed | tf_op | source)
XLA Modules:
  0.0 263.5 jit_solution(12890683117786738848)
XLA Ops:
  0.0 258.3 %shard_map.28.whole = bf16[2,8,38,80,128]{4,3,2,1,0:T(8,128)(2,1)S(1)} custom-call(bf16[4,4096,640]{2,1,0:T(8,128)(2,1)} %bitcast.3, bf16[4,4096,2432]{2,1,0:T(8,128)(2,1)} %bitcast.1.g_ref), custom_call_target="tpu_custom_call" | custom-call | flops 51002736640 | bytes 100663296 | tf_op jit(solution)/shard_map/pallas_call | solution.py:311
  258.4 5.2 %shard_map.29 = bf16[4,8,80,2432]{3,2,1,0:T(8,128)(2,1)} custom-call(bf16[2,8,38,80,128]{4,3,2,1,0:T(8,128)(2,1)S(1)} %shard_map.28.whole), custom_call_target="tpu_custom_call" | custom-call | tf_op jit(solution)/shard_map/pallas_call | solution.py:333

commit v4 on v3

--- a/solution.py
+++ b/solution.py
@@ -16,7 +16,7 @@
 MESH = pl.DeviceIdType.MESH
 
 
-def plan(groups, n, work=0.6, half=1.0, turn=0.36, load=0.66, lag=1.5, wire=0.44, gap=0.03,
+def plan(groups, n, work=0.55, half=0.95, turn=0.36, load=0.66, lag=1.5, wire=0.44, gap=0.03,
          depth=4.0):
     steps = 2 * n - 2
     ends = [sum(groups[:i + 1]) for i in range(len(groups))]
@@ -24,7 +24,6 @@
     pieces = [(r, p) for r in range(rounds) for p in range(FRONT)]
     pieces += [(h, p) for p in range(FRONT, ends[-1]) for h in range(2)]
     now, link, after, order, done = 0.0, 0.0, [], [], [0] * FRONT
-    held = {}
     x = 0
     while x < len(pieces) or after:
         ready = [e for e in after if e[0] <= now and (link - now < depth or e[1] == steps)
@@ -71,6 +70,7 @@
     last = 2 * n - 2
     begins = [sum(groups[:i]) for i in range(len(groups))]
     me = lax.axis_index("dp")
+    beside = (lax.rem(me + 1, n), lax.rem(me + n - 1, n))
 
     def owner(d, away):
         return lax.rem(me - (1 - 2 * d) * away + 2 * n, n)
@@ -158,39 +158,39 @@
 
     def carry(i, t):
         q, size = begins[i], groups[i]
-
-        def one(d, _):
-            def message_of(s):
-                return message(i, d, s, whole.at[d, 0, pl.ds(q, size)], me)
-
-            if t > 0:
-                message_of(t - 1).wait_recv()
-            c = owner(d, 1 + t if t < n else t - n + 1)
-            if t < n:
-                def add(j, _):
-                    term = part[q + j, d, at(c)]
+        c = [owner(d, 1 + t if t < n else t - n + 1) for d in range(2)]
+
+        def message_of(d, s):
+            return message(i, d, s, whole.at[d, 0, pl.ds(q, size)], me)
+
+        if t > 0:
+            for d in range(2):
+                message_of(d, t - 1).wait_recv()
+        if t < n:
+            def add(j, _):
+                for d in range(2):
+                    term = part[q + j, d, at(c[d])]
                     if t > 0:
-                        term = whole[d, c, q + j].astype(jnp.float32) + term
-                    whole[d, c, q + j] = term.astype(jnp.bfloat16)
-                    return 0
-
+                        term = whole[d, c[d], q + j].astype(jnp.float32) + term
+                    whole[d, c[d], q + j] = term.astype(jnp.bfloat16)
+                return 0
+
+            if size == 1:
+                add(0, 0)
+            else:
                 lax.fori_loop(0, size, add, 0)
+        for d in range(2):
             if t >= 2:
-                message_of(t - 2).wait_send()
+                message_of(d, t - 2).wait_send()
             if t < last:
-                to = lax.rem(me + 1 - 2 * d + n, n)
-                message(i, d, t, whole.at[d, c, pl.ds(q, size)], to).start()
+                message(i, d, t, whole.at[d, c[d], pl.ds(q, size)], beside[d]).start()
             else:
-                message_of(t - 1).wait_send()
-            return 0
-
-        lax.fori_loop(0, 2, one, 0)
+                message_of(d, t - 1).wait_send()
 
     for k in range(CHUNKS):
         a_copy(k).start()
     g_start(0)
     barrier = pltpu.get_barrier_semaphore()
-    beside = (lax.rem(me + 1, n), lax.rem(me + n - 1, n))
     for to in beside:
         pl.semaphore_signal(barrier, inc=1, device_id={"dp": to}, device_id_type=MESH)
 
@@ -284,19 +284,16 @@
 
 def put(n, whole, out_ref, sem):
     blocks = out_ref.shape[3] // LANES
-
-    def one(p, wait):
-        for d in range(2):
-            b = 2 * p + d
-            col = pl.multiple_of(lax.rem(b, blocks) * LANES, LANES)
-            copy = pltpu.make_async_copy(
-                whole.at[d, :, p], out_ref.at[b // blocks, :, :, pl.ds(col, LANES)],
-                sem.at[d, p])
-            copy.wait() if wait else copy.start()
-        return 0
-
-    lax.fori_loop(0, whole.shape[2], lambda p, _: one(p, False), 0)
-    lax.fori_loop(0, whole.shape[2], lambda p, _: one(p, True), 0)
+    copies = []
+    for b in range(2 * whole.shape[2]):
+        p, d = divmod(b, 2)
+        m, col = divmod(b, blocks)
+        copies.append(pltpu.make_async_copy(
+            whole.at[d, :, p], out_ref.at[m, :, :, pl.ds(col * LANES, LANES)], sem.at[d, p]))
+    for copy in copies:
+        copy.start()
+    for copy in copies:
+        copy.wait()
 
 
 def solution(mesh):

time: 264 us -> 263 us (level)
  no operation moved by 1% of the time
where the time goes in v4:
time: 263 us
  Pallas kernels  263 us (100%)
    pallas_call x1, Pallas kernels, local(): pl.pallas_call(functools.partial(kernel, n, GROUPS), out_shape=pltpu.VMEM...  258 us

profile of v4, /device:TPU:22, one launch (start us, length us, event | category | flops | bytes accessed | tf_op | source)
XLA Modules:
  0.0 263.1 jit_solution(708958645406027802)
XLA Ops:
  0.0 257.9 %shard_map.28.whole = bf16[2,8,38,80,128]{4,3,2,1,0:T(8,128)(2,1)S(1)} custom-call(bf16[4,4096,640]{2,1,0:T(8,128)(2,1)} %bitcast.3, bf16[4,4096,2432]{2,1,0:T(8,128)(2,1)} %bitcast.1.g_ref), custom_call_target="tpu_custom_call" | custom-call | flops 51002736640 | bytes 100663296 | tf_op jit(solution)/shard_map/pallas_call | solution.py:308
  257.9 5.1 %shard_map.29 = bf16[4,8,80,2432]{3,2,1,0:T(8,128)(2,1)} custom-call(bf16[2,8,38,80,128]{4,3,2,1,0:T(8,128)(2,1)S(1)} %shard_map.28.whole), custom_call_target="tpu_custom_call" | custom-call | tf_op jit(solution)/shard_map/pallas_call | solution.py:330
